TPU v7x, 32 devices: a whole 2x2x4 slice. The times are simulated.
32 devices in a mesh: dp: 8 (over y, x, core), tp: 4 (over z).
Axes of the slice: x: 2, y: 2, z: 4, core: 2. Of those that a mesh axis runs over, the one named last changes fastest.
Arguments:
- inputs: bfloat16 [8, 768, 1280], P('dp', 'tp'), may hold values from -6 to 6
- saved_hidden: bfloat16 [8, 768, 5120], P('dp', None, 'tp'), may hold values from -8 to 8
- upstream: bfloat16 [8, 768, 1280], P('dp', 'tp'), may hold values from -6 to 6
- w_in: bfloat16 [1280, 5120], P(None, 'tp'), may hold values from -0.15625 to 0.15625
- w_out: bfloat16 [5120, 1280], P('tp'), may hold values from -0.078125 to 0.078125
- kernel: float32 [7, 1280], replicated, may hold values from -2 to 2
Outputs:
- grad_inputs: bfloat16 [8, 768, 1280], P('dp', 'tp')
- grad_w_in: float32 [1280, 5120], P(None, 'tp')
- grad_w_out: float32 [5120, 1280], P('tp')
- grad_bias: float32 [5120], P('tp')
- grad_kernel: float32 [7, 1280], replicated
All inputs are finite; a program needn't handle non-finite values.
Results may differ from a plain program's by a relative error of at most 0.02.
Values may be sent and summed in bfloat16 or wider, within the bound.
No kernel may reach another device: no remote copies, remote signals or barrier semaphores. Data moves between devices by JAX's collectives and lax.ppermute only.
A program may use at most 128 MiB of HBM per device.

v0:
```python
import jax
import jax.numpy as jnp
from jax import lax
from jax.sharding import PartitionSpec as P

KW = 7


def with_halo(cells, sides, width):
    for axis, dim in sides:
        count = lax.axis_size(axis)
        ends = count - 1
        head = lax.slice_in_dim(cells, 0, width, axis=dim)
        tail = lax.slice_in_dim(cells, cells.shape[dim] - width, cells.shape[dim], axis=dim)
        cells = jnp.concatenate(
            [
                lax.ppermute(tail, axis, [(i, (i + 1) % count) for i in range(ends)]),
                cells,
                lax.ppermute(head, axis, [((i + 1) % count, i) for i in range(ends)]),
            ],
            axis=dim,
        )
    return cells


def gelu_exact(value):
    return jax.nn.gelu(value, approximate=False)


def convolve(padded, kernel, length):
    mixed = padded[3 : 3 + length].astype(jnp.float32)
    for tap in range(KW):
        mixed = mixed + kernel[tap] * padded[tap : tap + length].astype(jnp.float32)
    return mixed.astype(jnp.bfloat16)


def shards(inputs, saved_hidden, upstream, w_in, w_out, kernel):
    tokens = inputs[0]
    hidden = saved_hidden[0]
    grad_out = upstream[0]
    length = tokens.shape[0]
    piece = lax.all_gather(grad_out, "tp", axis=0, tiled=True)
    hidden_rows = hidden.astype(jnp.float32)
    back_rows = lax.dot_general(
        piece, w_out, (((1,), (1,)), ((), ())), preferred_element_type=jnp.float32
    )
    grad_rows = jax.vjp(gelu_exact, hidden_rows)[1](back_rows)[0].astype(jnp.bfloat16)
    buffer = grad_rows
    activated = gelu_exact(hidden_rows).astype(jnp.bfloat16)
    total = lax.dot_general(
        activated, piece, (((0,), (0,)), ((), ())), preferred_element_type=jnp.float32
    )
    grad_w_out = total
    grad_bias = jnp.sum(buffer.astype(jnp.float32), axis=0)
    summed = lax.psum_scatter(
        lax.dot_general(
            buffer, w_in, (((1,), (1,)), ((), ())), preferred_element_type=jnp.float32
        ).astype(jnp.bfloat16),
        "tp",
        scatter_dimension=0,
        tiled=True,
    ).astype(jnp.float32)
    grad_mixed = (grad_out.astype(jnp.float32) + summed).astype(jnp.bfloat16)
    padded = with_halo(tokens, (("tp", 0),), 3)
    mixed = convolve(padded, kernel, length)
    grad_rows = buffer
    grad_w_in = lax.dot_general(
        lax.all_gather(mixed, "tp", axis=0, tiled=True),
        grad_rows,
        (((0,), (0,)), ((), ())),
        preferred_element_type=jnp.float32,
    )
    grad_pad = with_halo(grad_mixed, (("tp", 0),), 3)
    grad_f = grad_mixed.astype(jnp.float32)
    grad_inputs = grad_f
    taps = []
    for tap in range(KW):
        grad_inputs = grad_inputs + kernel[tap] * grad_pad[6 - tap : 6 - tap + length].astype(
            jnp.float32
        )
        taps.append(jnp.sum(grad_f * padded[tap : tap + length].astype(jnp.float32), axis=0))
    grad_kernel = jnp.stack(taps)
    grad_kernel = lax.psum(grad_kernel, ("dp", "tp"))
    grad_w_in, grad_w_out, grad_bias = (
        lax.psum(grad_w_in.astype(jnp.bfloat16), "dp").astype(jnp.float32),
        lax.psum(grad_w_out.astype(jnp.bfloat16), "dp").astype(jnp.float32),
        lax.psum(grad_bias.astype(jnp.bfloat16), "dp").astype(jnp.float32),
    )
    return (grad_inputs.astype(jnp.bfloat16)[None], grad_w_in, grad_w_out, grad_bias, grad_kernel)


def solution(mesh):
    in_specs = (
        P("dp", "tp", None),
        P("dp", None, "tp"),
        P("dp", "tp", None),
        P(None, "tp"),
        P("tp", None),
        P(),
    )
    out_specs = (P("dp", "tp", None), P(None, "tp"), P("tp", None), P("tp"), P())
    return jax.shard_map(shards, mesh=mesh, in_specs=in_specs, out_specs=out_specs, check_vma=False)
```

profile of v0, /device:TPU:0, one launch (start us, length us, event | category | flops | bytes accessed | tf_op | source)
XLA Modules:
  0.0 318.5 jit_solution(17866380397956469389)
XLA Ops:
  7.2 0.0 all-gather.6.cloned.1.call-start
  7.2 0.7 all-gather.6.cloned.1.call-update
  7.9 0.0 all-gather.4.cloned.1.call-start
  8.0 1.0 slice_bitcast_fusion.1
  8.9 5.0 %collective-permute-start.2 = (bf16[3,1280]{1,0:T(4,128)(2,1)S(1)}, bf16[3,1280]{1,0:T(4,128)(2,1)S(1)}, u32[]{:S(2)}, u32[]{:S(2)}) collective-permute-start(bf16[3,1280]{1,0:T(4,128)(2,1)S(1)} %get-tuple-element.27), channel_id=1, source_target_pairs={{0,1},{1,2},{2,3},{4,5},{5,6},{6,7},{8,9},{9,10},{10,11},{12,13},{... | collective-permute-start | bytes 23048 | tf_op jit(solution)/shard_map/ppermute | solution.py:17
  13.9 1.3 collective-permute-start.3
  15.2 1.3 slice_reduce_fusion.6
  16.5 3.0 collective-permute-done.3
  19.4 4.4 %fusion.52 = bf16[192,1280]{1,0:T(8,128)(2,1)} fusion(bf16[192,1280]{1,0:T(8,128)(2,1)} %bitcast.131, bf16[3,1280]{1,0:T(4,128)(2,1)S(1)} %collective-permute-done.3, bf16[3,1280]{1,0:T(4,128)(2,1)S(1)} %collective-permute-done.2, f32[1280]{0:T(1024)S(1)} %get-tuple-element.20, f32[1280]{0:T(1024)S(1)} %get-tuple-element.21, f32[1280]{0:T(1024)S(1)} %get-tuple-element.16, ...), kind=kLoop, calls=%fused_computation.72 | loop fusion | flops 9830400 | bytes 1034240 | tf_op jit(solution)/shard_map/convert_element_type | solution.py:34
  23.8 0.0 all-gather.4.cloned.1.call-update
  23.9 0.0 all-reduce.3.cloned.1.call-start
  23.9 10.1 %fusion.38 = f32[768,1280]{1,0:T(8,128)} fusion(bf16[1,768,1280]{2,1,0:T(8,128)(2,1)} %param.7), kind=kLoop, calls=%fused_computation.43 | loop fusion | flops 61931520 | bytes 5898240 | tf_op jit(solution)/shard_map/jvp()/erfc | solution.py:27
  34.0 21.8 %all-gather.6.cloned.1.call-done = bf16[1,768,1280]{2,1,0:T(8,128)(2,1)} async-done(((bf16[1,192,1280]{2,1,0:T(8,128)(2,1)}), bf16[1,768,1280]{2,1,0:T(8,128)(2,1)}) %all-gather.6.cloned.1.call-update) | async-done | bytes 1966096 | tf_op jit(solution)/shard_map/all_gather | solution.py:42
  55.8 7.9 %convolution_convert_fusion = bf16[1280,1280]{1,0:T(8,128)(2,1)} fusion(f32[768,1280]{1,0:T(8,128)} %fusion.38, bf16[1,768,1280]{2,1,0:T(8,128)(2,1)} %param.7, bf16[1,768,1280]{2,1,0:T(8,128)(2,1)} %all-gather.6.cloned.1.call-done), kind=kOutput, calls=%fused_computation | convolution fusion | flops 2522152960 | bytes 11141120 | tf_op jit(solution)/shard_map/dot_general | solution.py:50
  63.8 4.7 %fusion.80 = (bf16[1280]{0:T(1024)(128)(2,1)S(1)}, bf16[768,1280]{1,0:T(8,128)(2,1)}) fusion(f32[768,1280]{1,0:T(8,128)S(1)} %copy-done.1, bf16[1280,1280]{1,0:T(8,128)(2,1)S(1)} %copy-done, bf16[1,768,1280]{2,1,0:T(8,128)(2,1)S(1)} %copy-done.5, bf16[1,768,1280]{2,1,0:T(8,128)(2,1)S(1)} %copy-done.4), kind=kOutput, calls=%fused_computation.121 | convolution fusion | flops 2532309760 | bytes 13109760 | tf_op jit(solution)/shard_map/dot_general | solution.py:44
  68.5 31.9 %all-gather.4.cloned.1.call-done = bf16[768,1280]{1,0:T(8,128)(2,1)} async-done(((bf16[192,1280]{1,0:T(8,128)(2,1)}), bf16[768,1280]{1,0:T(8,128)(2,1)}) %all-gather.4.cloned.1.call-update) | async-done | bytes 1966096 | tf_op jit(solution)/shard_map/all_gather | solution.py:68
  100.3 6.6 %convolution_convert_fusion.1 = bf16[1280,1280]{1,0:T(8,128)(2,1)} fusion(bf16[768,1280]{1,0:T(8,128)(2,1)} %all-gather.4.cloned.1.call-done, bf16[768,1280]{1,0:T(8,128)(2,1)} %get-tuple-element.30), kind=kOutput, calls=%fused_computation.1 | convolution fusion | flops 2518220800 | bytes 7208960 | tf_op jit(solution)/shard_map/dot_general | solution.py:67
  106.9 0.2 reduce-scatter.2.cloned.1.call-start
  107.2 6.6 %convolution_convert_fusion.2 = bf16[768,1280]{1,0:T(8,128)(2,1)} fusion(bf16[768,1280]{1,0:T(8,128)(2,1)} %get-tuple-element.30, bf16[1280,1280]{1,0:T(8,128)(2,1)} %param.9), kind=kOutput, calls=%fused_computation.44 | convolution fusion | flops 2517565440 | bytes 7208960 | tf_op jit(solution)/shard_map/dot_general | solution.py:56
  113.8 14.3 %psum.30 = bf16[1280]{0:T(1024)(128)(2,1)S(1)} all-reduce(bf16[1280]{0:T(1024)(128)(2,1)S(1)} %get-tuple-element.29), channel_id=1, replica_groups=mesh['dp'=8,'tp'=4] {'dp'}, use_global_device_ids=true, to_apply=%region_4.0 | all-reduce | flops 1280 | bytes 5120 | tf_op jit(solution)/shard_map/psum | solution.py:87
  128.1 0.6 convert_element_type.123
  128.7 84.3 %all-reduce.3.cloned.1.call-done = (bf16[1280,1280]{1,0:T(8,128)(2,1)}, bf16[1280,1280]{1,0:T(8,128)(2,1)}) async-done(((bf16[1280,1280]{1,0:T(8,128)(2,1)}, bf16[1280,1280]{1,0:T(8,128)(2,1)}), (bf16[1280,1280]{1,0:T(8,128)(2,1)}, bf16[1280,1280]{1,0:T(8,128)(2,1)})) %all-reduce.3.cloned.1.call-update) | async-done | bytes 6553616 | tf_op jit(solution)/shard_map/psum | solution.py:85
  213.1 5.4 %convert_element_type.119 = f32[1280,1280]{1,0:T(8,128)} convert(bf16[1280,1280]{1,0:T(8,128)(2,1)} %get-tuple-element.22) | non-fusion elementwise | flops 1638400 | bytes 9830400 | tf_op jit(solution)/shard_map/convert_element_type | solution.py:85
  218.4 3.3 %convert_element_type.122 = f32[1280,1280]{1,0:T(8,128)} convert(bf16[1280,1280]{1,0:T(8,128)(2,1)S(1)} %copy-done.2) | non-fusion elementwise | flops 1638400 | bytes 9830400 | tf_op jit(solution)/shard_map/convert_element_type | solution.py:86
  221.7 35.3 %reduce-scatter.2.cloned.1.call-done = bf16[192,1280]{1,0:T(8,128)(2,1)} async-done(((bf16[768,1280]{1,0:T(8,128)(2,1)}), bf16[192,1280]{1,0:T(8,128)(2,1)}) %reduce-scatter.2.cloned.1.call-update) | async-done | bytes 491536 | tf_op jit(solution)/shard_map/reduce_scatter | solution.py:55
  257.0 3.8 %fusion.66 = (f32[1280]{0:T(1024)S(1)}, f32[1280]{0:T(1024)S(1)}, f32[1280]{0:T(1024)S(1)}, f32[1280]{0:T(1024)S(1)}, f32[1280]{0:T(1024)S(1)}, /*index=5*/f32[1...) fusion(bf16[3,1280]{1,0:T(4,128)(2,1)S(1)} %collective-permute-done.3, bf16[192,1280]{1,0:T(8,128)(2,1)} %bitcast.132, ...), kind=kLoop, calls=%fused_computation.86 | loop fusion | flops 10804480 | bytes 2508800 | tf_op jit(solution)/shard_map/reduce_sum | solution.py:81
  260.9 0.7 copy-done.3
  261.6 1.3 collective-permute-start
  262.9 4.5 %collective-permute-start.1 = (bf16[3,1280]{1,0:T(4,128)(2,1)S(1)}, bf16[3,1280]{1,0:T(4,128)(2,1)S(1)}, u32[]{:S(2)}, u32[]{:S(2)}) collective-permute-start(bf16[3,1280]{1,0:T(4,128)(2,1)S(1)} %get-tuple-element.26), channel_id=1, source_target_pairs={{0,1},{1,2},{2,3},{4,5},{5,6},{6,7},{8,9},{9,10},{10,11},{12,13},{... | collective-permute-start | bytes 23048 | tf_op jit(solution)/shard_map/ppermute | solution.py:17
  267.4 0.1 stack.31
  267.5 40.2 %psum.31 = f32[7,1280]{1,0:T(8,128)} all-reduce(f32[7,1280]{1,0:T(8,128)S(1)} %stack.31), channel_id=1, replica_groups=mesh['dp'=8,'tp'=4] {'dp','tp'}, use_global_device_ids=true, to_apply=%region_12.0 | all-reduce | flops 8960 | bytes 71680 | tf_op jit(solution)/shard_map/psum | solution.py:83
  307.6 4.3 %fusion.76 = bf16[1,192,1280]{2,1,0:T(8,128)(2,1)} fusion(bf16[192,1280]{1,0:T(8,128)(2,1)} %copy-done.3, bf16[3,1280]{1,0:T(4,128)(2,1)S(1)} %collective-permute-done.1, f32[1280]{0:T(1024)S(1)} %get-tuple-element.20, f32[1280]{0:T(1024)S(1)} %get-tuple-element.21, f32[1280]{0:T(1024)S(1)} %get-tuple-element.16, f32[1280]{0:T(1024)S(1)} %get-tuple-element.17, ...), kind=kLoop, calls=%fused_computation.109 | loop fusion | flops 9830400 | bytes 1034240 | tf_op jit(solution)/shard_map/broadcast_in_dim | solution.py:89
  (24 shorter events, 0.1 us)
Async XLA Ops:
  7.2 56.6 %copy-start = (bf16[1280,1280]{1,0:T(8,128)(2,1)S(1)}, bf16[1280,1280]{1,0:T(8,128)(2,1)}, u32[]{:S(2)}) copy-start(bf16[1280,1280]{1,0:T(8,128)(2,1)} %param.10) | copy-start | bytes 9830404
  7.2 48.6 %all-gather.6.cloned.1.call-start = ((), (), s32[]{:S(2)}) async-start(), calls=%async_computation.3 | async-start | bytes 2457600 | tf_op jit(solution)/shard_map/all_gather | solution.py:42
  7.9 92.4 %all-gather.4.cloned.1.call-start = ((), (), s32[]{:S(2)}) async-start(), calls=%async_computation.2 | async-start | bytes 2457600 | tf_op jit(solution)/shard_map/all_gather | solution.py:68
  8.9 7.5 %collective-permute-start.2 = (bf16[3,1280]{1,0:T(4,128)(2,1)S(1)}, bf16[3,1280]{1,0:T(4,128)(2,1)S(1)}, u32[]{:S(2)}, u32[]{:S(2)}) collective-permute-start(bf16[3,1280]{1,0:T(4,128)(2,1)S(1)} %get-tuple-element.27), channel_id=1, source_target_pairs={{0,1},{1,2},{2,3},{4,5},{5,6},{6,7},{8,9},{9,10},{10,11},{12,13},{... | collective-permute-start | bytes 23048 | tf_op jit(solution)/shard_map/ppermute | solution.py:17
  13.9 5.6 %collective-permute-start.3 = (bf16[3,1280]{1,0:T(4,128)(2,1)S(1)}, bf16[3,1280]{1,0:T(4,128)(2,1)S(1)}, u32[]{:S(2)}, u32[]{:S(2)}) collective-permute-start(bf16[3,1280]{1,0:T(4,128)(2,1)S(1)} %get-tuple-element.28), channel_id=1, source_target_pairs={{1,0},{2,1},{3,2},{5,4},{6,5},{7,6},{9,8},{10,9},{11,10},{13,12},{... | collective-permute-start | bytes 23048 | tf_op jit(solution)/shard_map/ppermute | solution.py:19
  23.9 189.2 %all-reduce.3.cloned.1.call-start = ((), (), s32[]{:S(2)}) async-start(), calls=%async_computation.4 | async-start | bytes 13107200 | tf_op jit(solution)/shard_map/psum | solution.py:85
  55.8 7.9 %copy-start.1 = (f32[768,1280]{1,0:T(8,128)S(1)}, f32[768,1280]{1,0:T(8,128)}, u32[]{:S(2)}) copy-start(f32[768,1280]{1,0:T(8,128)} %fusion.38) | copy-start | bytes 11796484
  55.8 7.9 %copy-start.4 = (bf16[1,768,1280]{2,1,0:T(8,128)(2,1)S(1)}, bf16[1,768,1280]{2,1,0:T(8,128)(2,1)}, u32[]{:S(2)}) copy-start(bf16[1,768,1280]{2,1,0:T(8,128)(2,1)} %param.7) | copy-start | bytes 5898244
  55.8 7.9 %copy-start.5 = (bf16[1,768,1280]{2,1,0:T(8,128)(2,1)S(1)}, bf16[1,768,1280]{2,1,0:T(8,128)(2,1)}, u32[]{:S(2)}) copy-start(bf16[1,768,1280]{2,1,0:T(8,128)(2,1)} %all-gather.6.cloned.1.call-done) | copy-start | bytes 5898244
  106.9 150.0 %reduce-scatter.2.cloned.1.call-start = ((), (), s32[]{:S(2)}) async-start(), calls=%async_computation.1 | async-start | bytes 2457600 | tf_op jit(solution)/shard_map/reduce_scatter | solution.py:55
  213.1 5.4 %copy-start.2 = (bf16[1280,1280]{1,0:T(8,128)(2,1)S(1)}, bf16[1280,1280]{1,0:T(8,128)(2,1)}, u32[]{:S(2)}) copy-start(bf16[1280,1280]{1,0:T(8,128)(2,1)} %get-tuple-element.23) | copy-start | bytes 9830404
  260.8 0.8 copy-start.3
  261.6 46.1 %collective-permute-start = (bf16[3,1280]{1,0:T(4,128)(2,1)S(1)}, bf16[3,1280]{1,0:T(4,128)(2,1)S(1)}, u32[]{:S(2)}, u32[]{:S(2)}) collective-permute-start(bf16[3,1280]{1,0:T(4,128)(2,1)S(1)} %get-tuple-element.25), channel_id=1, source_target_pairs={{1,0},{2,1},{3,2},{5,4},{6,5},{7,6},{9,8},{10,9},{11,10},{13,12},{... | collective-permute-start | bytes 23048 | tf_op jit(solution)/shard_map/ppermute | solution.py:19
  262.9 44.8 %collective-permute-start.1 = (bf16[3,1280]{1,0:T(4,128)(2,1)S(1)}, bf16[3,1280]{1,0:T(4,128)(2,1)S(1)}, u32[]{:S(2)}, u32[]{:S(2)}) collective-permute-start(bf16[3,1280]{1,0:T(4,128)(2,1)S(1)} %get-tuple-element.26), channel_id=1, source_target_pairs={{0,1},{1,2},{2,3},{4,5},{5,6},{6,7},{8,9},{9,10},{10,11},{12,13},{... | collective-permute-start | bytes 23048 | tf_op jit(solution)/shard_map/ppermute | solution.py:17
Sparse Core Ops, SparseCore 0:
  9.6 46.2 all-gather.5
  58.0 42.3 all-gather.3
  107.1 105.9 all-reduce.2
  215.2 41.6 reduce-scatter.1
where the time goes:
time: 319 us; the launch traced here: 318 us
  waiting for transfers between devices  177 us (55%)
  blocking collectives  54.5 us (17%)
  other arithmetic  31.8 us (10%)
  matrix products  25.8 us (8%)
  between operations  13.9 us (4%)
  starting transfers between devices  12.4 us (4%)
    psum x1, waiting for transfers between devices, shards(): lax.psum(grad_w_in.astype(jnp.bfloat16), 'dp').astype(jnp.float32)  84.3 us
    psum x1, blocking collectives, shards(): grad_kernel = lax.psum(grad_kernel, ('dp', 'tp'))  40.2 us
    reduce_scatter x1, waiting for transfers between devices, shards(): lax.psum_scatter(lax.dot_general(buffer, w_in, (((1,), (1,)), ((), ())),...  35.3 us
    all_gather x1, waiting for transfers between devices, shards(): lax.all_gather(mixed, 'tp', axis=0, tiled=True)  31.9 us
    all_gather x1, waiting for transfers between devices, shards(): piece = lax.all_gather(grad_out, 'tp', axis=0, tiled=True)  21.8 us
    psum x1, blocking collectives, shards(): lax.psum(grad_bias.astype(jnp.bfloat16), 'dp').astype(jnp.float32)  14.3 us
    another operation x1, other arithmetic, gelu_exact(): return jax.nn.gelu(value, approximate=False)  10.1 us
    ppermute x2, starting transfers between devices, with_halo(): lax.ppermute(tail, axis, [(i, (i + 1) % count) for i in range(ends)])  9.5 us
  transfers between devices with their start and end apart: 8, of which 5 were waited for; matrix products, arithmetic and copies ran while one was open for 14% of the time, Pallas kernels for 0%

commit v1 on v0

--- a/solution.py
+++ b/solution.py
@@ -80,7 +80,7 @@
         )
         taps.append(jnp.sum(grad_f * padded[tap : tap + length].astype(jnp.float32), axis=0))
     grad_kernel = jnp.stack(taps)
-    grad_kernel = lax.psum(grad_kernel, ("dp", "tp"))
+    grad_kernel = lax.psum(lax.psum(grad_kernel, "tp"), "dp")
     grad_w_in, grad_w_out, grad_bias = (
         lax.psum(grad_w_in.astype(jnp.bfloat16), "dp").astype(jnp.float32),
         lax.psum(grad_w_out.astype(jnp.bfloat16), "dp").astype(jnp.float32),

time: 319 us -> 321 us (level)
    psum x1 -> x2, blocking collectives: 40.2 us -> 41 us  [shards(): grad_kernel = lax.psum(lax.psum(grad_kernel, 'tp'), 'dp')]
where the time goes in v1:
time: 321 us; the launch traced here: 320 us
  waiting for transfers between devices  177 us (55%)
  blocking collectives  55.3 us (17%)
  other arithmetic  32.5 us (10%)
  matrix products  25.8 us (8%)
  between operations  13.9 us (4%)
  starting transfers between devices  12.4 us (4%)
    psum x1, waiting for transfers between devices, shards(): lax.psum(grad_w_in.astype(jnp.bfloat16), 'dp').astype(jnp.float32)  84.3 us
    psum x2, blocking collectives, shards(): grad_kernel = lax.psum(lax.psum(grad_kernel, 'tp'), 'dp')  41 us
    reduce_scatter x1, waiting for transfers between devices, shards(): lax.psum_scatter(lax.dot_general(buffer, w_in, (((1,), (1,)), ((), ())),...  35.3 us
    all_gather x1, waiting for transfers between devices, shards(): lax.all_gather(mixed, 'tp', axis=0, tiled=True)  31.9 us
    all_gather x1, waiting for transfers between devices, shards(): piece = lax.all_gather(grad_out, 'tp', axis=0, tiled=True)  21.8 us
    psum x1, blocking collectives, shards(): lax.psum(grad_bias.astype(jnp.bfloat16), 'dp').astype(jnp.float32)  14.3 us
    another operation x1, other arithmetic, gelu_exact(): return jax.nn.gelu(value, approximate=False)  10.1 us
    ppermute x2, starting transfers between devices, with_halo(): lax.ppermute(tail, axis, [(i, (i + 1) % count) for i in range(ends)])  9.5 us
  transfers between devices with their start and end apart: 8, of which 5 were waited for; matrix products, arithmetic and copies ran while one was open for 14% of the time, Pallas kernels for 0%

profile of v1, /device:TPU:0, one launch (start us, length us, event | category | flops | bytes accessed | tf_op | source)
XLA Modules:
  0.0 320.1 jit_solution(2717562579214316680)
XLA Ops:
  7.2 0.0 all-gather.6.cloned.1.call-start
  7.2 0.7 all-gather.6.cloned.1.call-update
  7.9 0.0 all-gather.4.cloned.1.call-start
  8.0 1.0 slice_bitcast_fusion.1
  8.9 5.0 %collective-permute-start.2 = (bf16[3,1280]{1,0:T(4,128)(2,1)S(1)}, bf16[3,1280]{1,0:T(4,128)(2,1)S(1)}, u32[]{:S(2)}, u32[]{:S(2)}) collective-permute-start(bf16[3,1280]{1,0:T(4,128)(2,1)S(1)} %get-tuple-element.27), channel_id=1, source_target_pairs={{0,1},{1,2},{2,3},{4,5},{5,6},{6,7},{8,9},{9,10},{10,11},{12,13},{... | collective-permute-start | bytes 23048 | tf_op jit(solution)/shard_map/ppermute | solution.py:17
  13.9 1.3 collective-permute-start.3
  15.2 1.3 slice_reduce_fusion.6
  16.5 3.0 collective-permute-done.3
  19.4 4.4 %fusion.52 = bf16[192,1280]{1,0:T(8,128)(2,1)} fusion(bf16[192,1280]{1,0:T(8,128)(2,1)} %bitcast.131, bf16[3,1280]{1,0:T(4,128)(2,1)S(1)} %collective-permute-done.3, bf16[3,1280]{1,0:T(4,128)(2,1)S(1)} %collective-permute-done.2, f32[1280]{0:T(1024)S(1)} %get-tuple-element.20, f32[1280]{0:T(1024)S(1)} %get-tuple-element.21, f32[1280]{0:T(1024)S(1)} %get-tuple-element.16, ...), kind=kLoop, calls=%fused_computation.72 | loop fusion | flops 9830400 | bytes 1034240 | tf_op jit(solution)/shard_map/convert_element_type | solution.py:34
  23.9 0.0 all-reduce.3.cloned.1.call-start
  23.9 10.1 %fusion.38 = f32[768,1280]{1,0:T(8,128)} fusion(bf16[1,768,1280]{2,1,0:T(8,128)(2,1)} %param.7), kind=kLoop, calls=%fused_computation.43 | loop fusion | flops 61931520 | bytes 5898240 | tf_op jit(solution)/shard_map/jvp()/erfc | solution.py:27
  34.0 21.8 %all-gather.6.cloned.1.call-done = bf16[1,768,1280]{2,1,0:T(8,128)(2,1)} async-done(((bf16[1,192,1280]{2,1,0:T(8,128)(2,1)}), bf16[1,768,1280]{2,1,0:T(8,128)(2,1)}) %all-gather.6.cloned.1.call-update) | async-done | bytes 1966096 | tf_op jit(solution)/shard_map/all_gather | solution.py:42
  55.8 7.9 %convolution_convert_fusion = bf16[1280,1280]{1,0:T(8,128)(2,1)} fusion(f32[768,1280]{1,0:T(8,128)} %fusion.38, bf16[1,768,1280]{2,1,0:T(8,128)(2,1)} %param.7, bf16[1,768,1280]{2,1,0:T(8,128)(2,1)} %all-gather.6.cloned.1.call-done), kind=kOutput, calls=%fused_computation | convolution fusion | flops 2522152960 | bytes 11141120 | tf_op jit(solution)/shard_map/dot_general | solution.py:50
  63.8 4.7 %fusion.80 = (bf16[1280]{0:T(1024)(128)(2,1)S(1)}, bf16[768,1280]{1,0:T(8,128)(2,1)}) fusion(f32[768,1280]{1,0:T(8,128)S(1)} %copy-done.1, bf16[1280,1280]{1,0:T(8,128)(2,1)S(1)} %copy-done, bf16[1,768,1280]{2,1,0:T(8,128)(2,1)S(1)} %copy-done.4, bf16[1,768,1280]{2,1,0:T(8,128)(2,1)S(1)} %copy-done.3), kind=kOutput, calls=%fused_computation.121 | convolution fusion | flops 2532309760 | bytes 13109760 | tf_op jit(solution)/shard_map/dot_general | solution.py:44
  68.5 31.9 %all-gather.4.cloned.1.call-done = bf16[768,1280]{1,0:T(8,128)(2,1)} async-done(((bf16[192,1280]{1,0:T(8,128)(2,1)}), bf16[768,1280]{1,0:T(8,128)(2,1)}) %all-gather.4.cloned.1.call-update) | async-done | bytes 1966096 | tf_op jit(solution)/shard_map/all_gather | solution.py:68
  100.3 6.6 %convolution_convert_fusion.1 = bf16[1280,1280]{1,0:T(8,128)(2,1)} fusion(bf16[768,1280]{1,0:T(8,128)(2,1)} %all-gather.4.cloned.1.call-done, bf16[768,1280]{1,0:T(8,128)(2,1)} %get-tuple-element.30), kind=kOutput, calls=%fused_computation.1 | convolution fusion | flops 2518220800 | bytes 7208960 | tf_op jit(solution)/shard_map/dot_general | solution.py:67
  106.9 0.2 reduce-scatter.2.cloned.1.call-start
  107.2 6.6 %convolution_convert_fusion.2 = bf16[768,1280]{1,0:T(8,128)(2,1)} fusion(bf16[768,1280]{1,0:T(8,128)(2,1)} %get-tuple-element.30, bf16[1280,1280]{1,0:T(8,128)(2,1)} %param.9), kind=kOutput, calls=%fused_computation.44 | convolution fusion | flops 2517565440 | bytes 7208960 | tf_op jit(solution)/shard_map/dot_general | solution.py:56
  113.8 14.3 %psum.37 = bf16[1280]{0:T(1024)(128)(2,1)S(1)} all-reduce(bf16[1280]{0:T(1024)(128)(2,1)S(1)} %get-tuple-element.29), channel_id=1, replica_groups=mesh['dp'=8,'tp'=4] {'dp'}, use_global_device_ids=true, to_apply=%region_4.0 | all-reduce | flops 1280 | bytes 5120 | tf_op jit(solution)/shard_map/psum | solution.py:87
  128.1 0.6 convert_element_type.123
  128.7 84.3 %all-reduce.3.cloned.1.call-done = (bf16[1280,1280]{1,0:T(8,128)(2,1)}, bf16[1280,1280]{1,0:T(8,128)(2,1)}) async-done(((bf16[1280,1280]{1,0:T(8,128)(2,1)}, bf16[1280,1280]{1,0:T(8,128)(2,1)}), (bf16[1280,1280]{1,0:T(8,128)(2,1)}, bf16[1280,1280]{1,0:T(8,128)(2,1)})) %all-reduce.3.cloned.1.call-update) | async-done | bytes 6553616 | tf_op jit(solution)/shard_map/psum | solution.py:85
  213.1 5.4 %convert_element_type.119 = f32[1280,1280]{1,0:T(8,128)} convert(bf16[1280,1280]{1,0:T(8,128)(2,1)} %get-tuple-element.22) | non-fusion elementwise | flops 1638400 | bytes 9830400 | tf_op jit(solution)/shard_map/convert_element_type | solution.py:85
  218.4 3.3 %convert_element_type.122 = f32[1280,1280]{1,0:T(8,128)} convert(bf16[1280,1280]{1,0:T(8,128)(2,1)S(1)} %copy-done.2) | non-fusion elementwise | flops 1638400 | bytes 9830400 | tf_op jit(solution)/shard_map/convert_element_type | solution.py:86
  221.7 35.3 %reduce-scatter.2.cloned.1.call-done = bf16[192,1280]{1,0:T(8,128)(2,1)} async-done(((bf16[768,1280]{1,0:T(8,128)(2,1)}), bf16[192,1280]{1,0:T(8,128)(2,1)}) %reduce-scatter.2.cloned.1.call-update) | async-done | bytes 491536 | tf_op jit(solution)/shard_map/reduce_scatter | solution.py:55
  257.0 4.4 %fusion.66 = (f32[1280]{0:T(1024)S(1)}, f32[1280]{0:T(1024)S(1)}, f32[1280]{0:T(1024)S(1)}, f32[1280]{0:T(1024)S(1)}, f32[1280]{0:T(1024)S(1)}, /*index=5*/f32[1...) fusion(bf16[3,1280]{1,0:T(4,128)(2,1)S(1)} %collective-permute-done.3, bf16[192,1280]{1,0:T(8,128)(2,1)} %bitcast.132, ...), kind=kLoop, calls=%fused_computation.86 | loop fusion | flops 10804480 | bytes 2508800 | tf_op jit(solution)/shard_map/reduce_sum | solution.py:81
  261.5 0.1 stack.31
  261.6 17.7 %psum.38 = f32[7,1280]{1,0:T(8,128)S(1)} all-reduce(f32[7,1280]{1,0:T(8,128)S(1)} %stack.31), channel_id=1, replica_groups=mesh['dp'=8,'tp'=4] {'tp'}, use_global_device_ids=true, to_apply=%region_12.0 | all-reduce | flops 8960 | bytes 71680 | tf_op jit(solution)/shard_map/psum | solution.py:83
  279.3 0.8 fusion.79
  280.1 1.3 collective-permute-start
  281.4 4.5 %collective-permute-start.1 = (bf16[3,1280]{1,0:T(4,128)(2,1)S(1)}, bf16[3,1280]{1,0:T(4,128)(2,1)S(1)}, u32[]{:S(2)}, u32[]{:S(2)}) collective-permute-start(bf16[3,1280]{1,0:T(4,128)(2,1)S(1)} %get-tuple-element.26), channel_id=1, source_target_pairs={{0,1},{1,2},{2,3},{4,5},{5,6},{6,7},{8,9},{9,10},{10,11},{12,13},{... | collective-permute-start | bytes 23048 | tf_op jit(solution)/shard_map/ppermute | solution.py:17
  285.9 23.3 %psum.39 = f32[7,1280]{1,0:T(8,128)} all-reduce(f32[7,1280]{1,0:T(8,128)S(1)} %psum.38), channel_id=1, replica_groups=mesh['dp'=8,'tp'=4] {'dp'}, use_global_device_ids=true, to_apply=%region_13.0 | all-reduce | flops 8960 | bytes 71680 | tf_op jit(solution)/shard_map/psum | solution.py:83
  309.2 4.3 %fusion.76 = bf16[1,192,1280]{2,1,0:T(8,128)(2,1)} fusion(bf16[192,1280]{1,0:T(8,128)(2,1)} %get-tuple-element.24, bf16[3,1280]{1,0:T(4,128)(2,1)S(1)} %collective-permute-done.1, f32[1280]{0:T(1024)S(1)} %get-tuple-element.20, f32[1280]{0:T(1024)S(1)} %get-tuple-element.21, f32[1280]{0:T(1024)S(1)} %get-tuple-element.16, f32[1280]{0:T(1024)S(1)} %get-tuple-element.17, ...), kind=kLoop, calls=%fused_computation.109 | loop fusion | flops 9830400 | bytes 1034240 | tf_op jit(solution)/shard_map/broadcast_in_dim | solution.py:89
  (23 shorter events, 0.1 us)
Async XLA Ops:
  7.2 56.6 %copy-start = (bf16[1280,1280]{1,0:T(8,128)(2,1)S(1)}, bf16[1280,1280]{1,0:T(8,128)(2,1)}, u32[]{:S(2)}) copy-start(bf16[1280,1280]{1,0:T(8,128)(2,1)} %param.10) | copy-start | bytes 9830404
  7.2 48.6 %all-gather.6.cloned.1.call-start = ((), (), s32[]{:S(2)}) async-start(), calls=%async_computation.3 | async-start | bytes 2457600 | tf_op jit(solution)/shard_map/all_gather | solution.py:42
  7.9 92.4 %all-gather.4.cloned.1.call-start = ((), (), s32[]{:S(2)}) async-start(), calls=%async_computation.2 | async-start | bytes 2457600 | tf_op jit(solution)/shard_map/all_gather | solution.py:68
  8.9 7.5 %collective-permute-start.2 = (bf16[3,1280]{1,0:T(4,128)(2,1)S(1)}, bf16[3,1280]{1,0:T(4,128)(2,1)S(1)}, u32[]{:S(2)}, u32[]{:S(2)}) collective-permute-start(bf16[3,1280]{1,0:T(4,128)(2,1)S(1)} %get-tuple-element.27), channel_id=1, source_target_pairs={{0,1},{1,2},{2,3},{4,5},{5,6},{6,7},{8,9},{9,10},{10,11},{12,13},{... | collective-permute-start | bytes 23048 | tf_op jit(solution)/shard_map/ppermute | solution.py:17
  13.9 5.6 %collective-permute-start.3 = (bf16[3,1280]{1,0:T(4,128)(2,1)S(1)}, bf16[3,1280]{1,0:T(4,128)(2,1)S(1)}, u32[]{:S(2)}, u32[]{:S(2)}) collective-permute-start(bf16[3,1280]{1,0:T(4,128)(2,1)S(1)} %get-tuple-element.28), channel_id=1, source_target_pairs={{1,0},{2,1},{3,2},{5,4},{6,5},{7,6},{9,8},{10,9},{11,10},{13,12},{... | collective-permute-start | bytes 23048 | tf_op jit(solution)/shard_map/ppermute | solution.py:19
  23.9 189.2 %all-reduce.3.cloned.1.call-start = ((), (), s32[]{:S(2)}) async-start(), calls=%async_computation.4 | async-start | bytes 13107200 | tf_op jit(solution)/shard_map/psum | solution.py:85
  55.8 7.9 %copy-start.1 = (f32[768,1280]{1,0:T(8,128)S(1)}, f32[768,1280]{1,0:T(8,128)}, u32[]{:S(2)}) copy-start(f32[768,1280]{1,0:T(8,128)} %fusion.38) | copy-start | bytes 11796484
  55.8 7.9 %copy-start.3 = (bf16[1,768,1280]{2,1,0:T(8,128)(2,1)S(1)}, bf16[1,768,1280]{2,1,0:T(8,128)(2,1)}, u32[]{:S(2)}) copy-start(bf16[1,768,1280]{2,1,0:T(8,128)(2,1)} %param.7) | copy-start | bytes 5898244
  55.8 7.9 %copy-start.4 = (bf16[1,768,1280]{2,1,0:T(8,128)(2,1)S(1)}, bf16[1,768,1280]{2,1,0:T(8,128)(2,1)}, u32[]{:S(2)}) copy-start(bf16[1,768,1280]{2,1,0:T(8,128)(2,1)} %all-gather.6.cloned.1.call-done) | copy-start | bytes 5898244
  106.9 150.0 %reduce-scatter.2.cloned.1.call-start = ((), (), s32[]{:S(2)}) async-start(), calls=%async_computation.1 | async-start | bytes 2457600 | tf_op jit(solution)/shard_map/reduce_scatter | solution.py:55
  213.1 5.4 %copy-start.2 = (bf16[1280,1280]{1,0:T(8,128)(2,1)S(1)}, bf16[1280,1280]{1,0:T(8,128)(2,1)}, u32[]{:S(2)}) copy-start(bf16[1280,1280]{1,0:T(8,128)(2,1)} %get-tuple-element.23) | copy-start | bytes 9830404
  280.1 29.2 %collective-permute-start = (bf16[3,1280]{1,0:T(4,128)(2,1)S(1)}, bf16[3,1280]{1,0:T(4,128)(2,1)S(1)}, u32[]{:S(2)}, u32[]{:S(2)}) collective-permute-start(bf16[3,1280]{1,0:T(4,128)(2,1)S(1)} %get-tuple-element.25), channel_id=1, source_target_pairs={{1,0},{2,1},{3,2},{5,4},{6,5},{7,6},{9,8},{10,9},{11,10},{13,12},{... | collective-permute-start | bytes 23048 | tf_op jit(solution)/shard_map/ppermute | solution.py:19
  281.4 27.9 %collective-permute-start.1 = (bf16[3,1280]{1,0:T(4,128)(2,1)S(1)}, bf16[3,1280]{1,0:T(4,128)(2,1)S(1)}, u32[]{:S(2)}, u32[]{:S(2)}) collective-permute-start(bf16[3,1280]{1,0:T(4,128)(2,1)S(1)} %get-tuple-element.26), channel_id=1, source_target_pairs={{0,1},{1,2},{2,3},{4,5},{5,6},{6,7},{8,9},{9,10},{10,11},{12,13},{... | collective-permute-start | bytes 23048 | tf_op jit(solution)/shard_map/ppermute | solution.py:17
Sparse Core Ops, SparseCore 0:
  9.6 46.2 all-gather.5
  58.0 42.3 all-gather.3
  107.1 105.9 all-reduce.2
  215.2 41.6 reduce-scatter.1
